TPU v7x, 32 devices: a whole 2x2x4 slice. The times are simulated.
32 devices in a mesh: dp: 4 (over x, core), mp: 8 (over z, y).
Axes of the slice: x: 2, y: 2, z: 4, core: 2. Of those that a mesh axis runs over, the one named last changes fastest.
Arguments:
- tokens: bfloat16 [1024, 8192], P('dp'), may hold values from -6 to 6
- norm_gain: float32 [8192], replicated, may hold values from 0.5 to 1.5
- gate_weight: bfloat16 [8192, 28672], P('dp', 'mp'), may hold values from -0.0625 to 0.0625
- gate_mask: int32 [8192, 896], P('dp', 'mp'), may hold values from -2147483648 to 2147483646
- up_weight: bfloat16 [8192, 28672], P('dp', 'mp'), may hold values from -0.0625 to 0.0625
- up_mask: int32 [8192, 896], P('dp', 'mp'), may hold values from -2147483648 to 2147483646
- down_weight: bfloat16 [28672, 8192], P('mp', 'dp'), may hold values from -0.03125 to 0.03125
- down_mask: int32 [28672, 256], P('mp', 'dp'), may hold values from -2147483648 to 2147483647, as said below
Outputs:
- mixed: bfloat16 [1024, 8192], P('mp', 'dp')
- input_norms: float32 [8192], P('dp')
- hidden_norms: float32 [28672], P('mp')
Inputs may be any that keep to these rules, and one draw needn't show every extreme that they name: `down_mask`: in every word each of the eight aligned groups of four bits holds exactly two ones, so exactly two of every four consecutive columns of the down projection are kept.
All inputs are finite; a program needn't handle non-finite values.
Results may differ from a plain program's by a relative error of at most 0.025.
Values may be sent and summed in bfloat16 or wider, within the bound.
A program may use at most 192 MiB of HBM per device.

v0:
```python
import jax
import jax.numpy as jnp
from jax import lax
from jax.sharding import PartitionSpec as P


def keep_entries(weight, packed):
    shifts = jnp.arange(32, dtype=jnp.int32)
    kept_bits = jnp.right_shift(packed[..., None], shifts) & 1
    kept_bits = kept_bits.reshape(weight.shape)
    return jnp.where(kept_bits == 1, weight, jnp.zeros_like(weight))


def on_device(
    tokens, norm_gain, gate_weight, gate_mask, up_weight, up_mask, down_weight, down_mask
):
    values = tokens.astype(jnp.float32)
    scale = lax.rsqrt(jnp.mean(values * values, axis=1, keepdims=True) + 1e-05)
    normed = (values * scale * norm_gain).astype(jnp.bfloat16)
    columns = lax.all_to_all(normed, "dp", split_axis=1, concat_axis=0, tiled=True)
    widened = columns.astype(jnp.float32)
    input_norms = jnp.sqrt(jnp.sum(widened * widened, axis=0))
    gate_kept = keep_entries(gate_weight, gate_mask)
    up_kept = keep_entries(up_weight, up_mask)
    down_kept = keep_entries(down_weight, down_mask)
    units = gate_kept.shape[1]
    gate_part = jnp.dot(columns, gate_kept, preferred_element_type=jnp.float32)
    up_part = jnp.dot(columns, up_kept, preferred_element_type=jnp.float32)
    both_sums = lax.psum_scatter(
        jnp.concatenate([gate_part, up_part], axis=1).astype(jnp.bfloat16),
        "dp",
        scatter_dimension=0,
        tiled=True,
    ).astype(jnp.float32)
    hidden = (jax.nn.silu(both_sums[:, :units]) * both_sums[:, units:]).astype(jnp.bfloat16)
    wide_hidden = hidden.astype(jnp.float32)
    squares = lax.psum(jnp.sum(wide_hidden * wide_hidden, axis=0), "dp")
    hidden_norms = jnp.sqrt(squares)
    partial_out = jnp.dot(
        lax.all_gather(hidden, "dp", axis=0, tiled=True),
        down_kept,
        preferred_element_type=jnp.float32,
    )
    mixed = lax.psum_scatter(
        partial_out.astype(jnp.bfloat16), "mp", scatter_dimension=0, tiled=True
    )
    return (mixed, input_norms, hidden_norms)


def solution(mesh):
    return jax.shard_map(
        on_device,
        mesh=mesh,
        in_specs=(
            P("dp", None),
            P(),
            P("dp", "mp"),
            P("dp", "mp"),
            P("dp", "mp"),
            P("dp", "mp"),
            P("mp", "dp"),
            P("mp", "dp"),
        ),
        out_specs=(P("mp", "dp"), P("dp"), P("mp")),
        check_vma=False,
    )
```

profile of v0, /device:TPU:0, one launch (start us, length us, event | category | flops | bytes accessed | tf_op | source)
XLA Modules:
  0.0 449.8 jit_solution(9891590436069383037)
XLA Ops:
  7.2 0.0 copy-start.4
  7.2 6.4 %copy.17 = bf16[256,8192]{0,1:T(8,128)(2,1)} copy(bf16[256,8192]{1,0:T(8,128)(2,1)} %param.8) | data formatting | bytes 8388608 | tf_op args[0]
  13.6 3.3 fusion.9
  16.9 0.0 copy-done.4
  16.9 4.2 fusion.11
  21.0 4.9 %all-to-all-start = ((bf16[256,4,2048]{0,2,1:T(8,128)(2,1)}), bf16[256,4,2048]{0,2,1:T(8,128)(2,1)}, u32[]{:S(2)}, u32[]{:S(2)}) async-start(bf16[256,4,2048]{0,2,1:T(8,128)(2,1)} %bitcast.34), calls=%async_computation | async-start | bytes 8388608 | tf_op jit(solution)/shard_map/all_to_all | solution.py:20
  25.9 0.0 reduce-scatter.3.cloned.1.call-start
  26.0 0.1 shift_right_arithmetic.63
  26.1 20.3 %copy.19 = bf16[2048,3584]{0,1:T(8,128)(2,1)} copy(bf16[2048,3584]{1,0:T(8,128)(2,1)} %param.10) | data formatting | bytes 29360128 | tf_op args[2]
  46.4 0.0 copy-start.1
  46.4 0.0 copy-start.2
  46.4 20.5 %copy.20 = bf16[2048,3584]{0,1:T(8,128)(2,1)} copy(bf16[2048,3584]{1,0:T(8,128)(2,1)} %param.12) | data formatting | bytes 29360128 | tf_op args[4]
  66.9 0.0 copy-done.1
  66.9 0.0 copy-done.2
  66.9 28.4 %fusion.6 = (bf16[2048,3584]{0,1:T(8,128)(2,1)}, bf16[2048,3584]{0,1:T(8,128)(2,1)}) fusion(bf16[2048,3584]{0,1:T(8,128)(2,1)} %copy.19, s32[3584]{0:T(1024)S(1)} %shift_right_arithmetic.63, s32[2048,112]{0,1:T(8,128)S(1)} %copy-done.1, bf16[2048,3584]{0,1:T(8,128)(2,1)} %copy.20, s32[2048,112]{0,1:T(8,128)S(1)} %copy-done.2), kind=kLoop, calls=%fused_computation.9 | loop fusion | flops 58720256 | bytes 60569600 | tf_op jit(solution)/shard_map/jit(_where)/select_n | solution.py:11
  95.3 0.0 all-to-all-done
  95.3 6.3 %copy.18 = bf16[4,256,2048]{2,1,0:T(8,128)(2,1)} copy(bf16[4,256,2048]{1,2,0:T(8,128)(2,1)} %bitcast.1) | data formatting | bytes 8388608 | tf_op jit(solution)/shard_map/all_to_all | solution.py:20
  101.6 0.0 copy-start
  101.6 23.7 %convolution_convert_fusion.1 = bf16[1024,3584]{1,0:T(8,128)(2,1)} fusion(bf16[1024,2048]{1,0:T(8,128)(2,1)} %bitcast.35, bf16[2048,3584]{0,1:T(8,128)(2,1)} %get-tuple-element.5), kind=kOutput, calls=%fused_computation.20 | convolution fusion | flops 15036055552 | bytes 26214400 | tf_op jit(solution)/shard_map/dot_general | solution.py:27
  125.3 0.0 copy-done
  125.3 20.5 %convolution_convert_fusion = bf16[1024,3584]{1,0:T(8,128)(2,1)} fusion(bf16[1024,2048]{1,0:T(8,128)(2,1)S(1)} %bitcast.36, bf16[2048,3584]{0,1:T(8,128)(2,1)} %get-tuple-element.6), kind=kOutput, calls=%fused_computation.19 | convolution fusion | flops 15036055552 | bytes 26214400 | tf_op jit(solution)/shard_map/dot_general | solution.py:28
  145.8 12.6 %pad_maximum_fusion = bf16[1024,7168]{1,0:T(8,128)(2,1)} fusion(bf16[1024,3584]{1,0:T(8,128)(2,1)} %convolution_convert_fusion, bf16[1024,3584]{1,0:T(8,128)(2,1)} %convolution_convert_fusion.1), kind=kLoop, calls=%fused_computation.12 | loop fusion | flops 29360128 | bytes 29360128 | tf_op jit(solution)/shard_map/concatenate | solution.py:30
  158.4 0.0 reduce-scatter.3.cloned.1.call-update
  158.5 0.0 all-gather.2.cloned.1.call-start
  158.5 117.2 %reduce-scatter.3.cloned.1.call-done = bf16[256,7168]{1,0:T(8,128)(2,1)} async-done(((bf16[1024,7168]{1,0:T(8,128)(2,1)}), bf16[256,7168]{1,0:T(8,128)(2,1)}) %reduce-scatter.3.cloned.1.call-update) | async-done | bytes 3670032 | tf_op jit(solution)/shard_map/reduce_scatter | solution.py:29
  275.7 2.9 convert_element_type.25
  278.6 2.5 multiply_reduce_fusion.1
  281.2 0.0 all-gather.2.cloned.1.call-update
  281.2 0.0 reduce-scatter.5.cloned.1.call-start
  281.2 0.1 shift_right_arithmetic.72
  281.3 0.0 copy-start.3
  281.3 19.5 %copy.21 = bf16[3584,2048]{0,1:T(8,128)(2,1)} copy(bf16[3584,2048]{1,0:T(8,128)(2,1)} %param.14) | data formatting | bytes 29360128 | tf_op args[6]
  300.8 0.0 copy-done.3
  300.8 15.1 %fusion.8 = bf16[3584,2048]{0,1:T(8,128)(2,1)} fusion(bf16[3584,2048]{0,1:T(8,128)(2,1)} %copy.21, s32[2048]{0:T(1024)S(1)} %shift_right_arithmetic.72, s32[3584,64]{0,1:T(8,128)S(1)} %copy-done.3), kind=kLoop, calls=%fused_computation.11 | loop fusion | flops 29360128 | bytes 30285824 | tf_op jit(solution)/shard_map/jit(_where)/select_n | solution.py:11
  315.9 17.7 %all-gather.2.cloned.1.call-done = bf16[1024,3584]{1,0:T(8,128)(2,1)} async-done(((bf16[256,3584]{1,0:T(8,128)(2,1)}), bf16[1024,3584]{1,0:T(8,128)(2,1)}) %all-gather.2.cloned.1.call-update) | async-done | bytes 7340048 | tf_op jit(solution)/shard_map/all_gather | solution.py:40
  333.6 21.2 %convolution_convert_fusion.2 = bf16[1024,2048]{1,0:T(8,128)(2,1)} fusion(bf16[1024,3584]{1,0:T(8,128)(2,1)} %all-gather.2.cloned.1.call-done, bf16[3584,2048]{0,1:T(8,128)(2,1)} %fusion.8), kind=kOutput, calls=%fused_computation.21 | convolution fusion | flops 15034482688 | bytes 26214400 | tf_op jit(solution)/shard_map/dot_general | solution.py:39
  354.8 0.0 reduce-scatter.5.cloned.1.call-update
  354.9 3.1 multiply_reduce_fusion
  357.9 0.6 sqrt.6
  358.6 10.6 %psum.7 = f32[3584]{0:T(1024)S(1)} all-reduce(f32[3584]{0:T(1024)S(1)} %get-tuple-element.3), channel_id=1, replica_groups=mesh['dp'=4,'mp'=8] {'dp'}, use_global_device_ids=true, to_apply=%region_5.6 | all-reduce | flops 3584 | bytes 28672 | tf_op jit(solution)/shard_map/psum | solution.py:37
  369.2 0.6 sqrt.7
  369.8 73.5 %reduce-scatter.5.cloned.1.call-done = bf16[128,2048]{1,0:T(8,128)(2,1)} async-done(((bf16[1024,2048]{1,0:T(8,128)(2,1)}), bf16[128,2048]{1,0:T(8,128)(2,1)}) %reduce-scatter.5.cloned.1.call-update) | async-done | bytes 524304 | tf_op jit(solution)/shard_map/reduce_scatter | solution.py:44
  (3 shorter events, 0.0 us)
Async XLA Ops:
  7.2 9.7 %copy-start.4 = (f32[8192]{0:T(1024)S(1)}, f32[8192]{0:T(1024)}, u32[]{:S(2)}) copy-start(f32[8192]{0:T(1024)} %param.9) | copy-start | bytes 98308
  21.0 74.2 %all-to-all-start = ((bf16[256,4,2048]{0,2,1:T(8,128)(2,1)}), bf16[256,4,2048]{0,2,1:T(8,128)(2,1)}, u32[]{:S(2)}, u32[]{:S(2)}) async-start(bf16[256,4,2048]{0,2,1:T(8,128)(2,1)} %bitcast.34), calls=%async_computation | async-start | bytes 8388608 | tf_op jit(solution)/shard_map/all_to_all | solution.py:20
  25.9 249.8 %reduce-scatter.3.cloned.1.call-start = ((), (), s32[]{:S(2)}) async-start(), calls=%async_computation.3 | async-start | bytes 18350080 | tf_op jit(solution)/shard_map/reduce_scatter | solution.py:29
  46.4 20.5 %copy-start.1 = (s32[2048,112]{0,1:T(8,128)S(1)}, s32[2048,112]{0,1:T(8,128)}, u32[]{:S(2)}) copy-start(s32[2048,112]{0,1:T(8,128)} %param.11) | copy-start | bytes 2752516
  46.4 20.5 %copy-start.2 = (s32[2048,112]{0,1:T(8,128)S(1)}, s32[2048,112]{0,1:T(8,128)}, u32[]{:S(2)}) copy-start(s32[2048,112]{0,1:T(8,128)} %param.13) | copy-start | bytes 2752516
  101.6 23.7 %copy-start = (bf16[4,256,2048]{2,1,0:T(8,128)(2,1)S(1)}, bf16[4,256,2048]{2,1,0:T(8,128)(2,1)}, u32[]{:S(2)}) copy-start(bf16[4,256,2048]{2,1,0:T(8,128)(2,1)} %copy.18) | copy-start | bytes 12582916
  158.5 175.2 %all-gather.2.cloned.1.call-start = ((), (), s32[]{:S(2)}) async-start(), calls=%async_computation.4 | async-start | bytes 9175040 | tf_op jit(solution)/shard_map/all_gather | solution.py:40
  281.2 162.1 %reduce-scatter.5.cloned.1.call-start = ((), (), s32[]{:S(2)}) async-start(), calls=%async_computation.5 | async-start | bytes 4718592 | tf_op jit(solution)/shard_map/reduce_scatter | solution.py:44
  281.3 19.5 %copy-start.3 = (s32[3584,64]{0,1:T(8,128)S(1)}, s32[3584,64]{0,1:T(8,128)}, u32[]{:S(2)}) copy-start(s32[3584,64]{0,1:T(8,128)} %param.15) | copy-start | bytes 2752516
Sparse Core Ops, SparseCore 0:
  158.6 117.0 reduce-scatter.2
  281.3 52.2 all-gather.1
  355.0 88.2 reduce-scatter.4
where the time goes:
time: 452 us; the launch traced here: 450 us
  waiting for transfers between devices  208 us (46%)
  local copies, waits for them, and re-layouts  74.5 us (16%)
  other arithmetic  72 us (16%)
  matrix products  65.4 us (14%)
  between operations  13.8 us (3%)
  blocking collectives  10.6 us (2%)
  starting transfers between devices  5.01 us (1%)
    reduce_scatter x1, waiting for transfers between devices, on_device(): lax.psum_scatter(jnp.concatenate([gate_part, up_part], axis=1).astype(jnp...  117 us
    reduce_scatter x1, waiting for transfers between devices, on_device(): lax.psum_scatter(partial_out.astype(jnp.bfloat16), 'mp', scatter_dimensio...  73.5 us
    unnamed x14, local copies, waits for them, and re-layouts  66.7 us
    select_n x2, other arithmetic, keep_entries(): return jnp.where(kept_bits == 1, weight, jnp.zeros_like(weight))  43.5 us
    dot_general x1, matrix products, on_device(): gate_part = jnp.dot(columns, gate_kept, preferred_element_type=jnp.float32)  23.7 us
    dot_general x1, matrix products, on_device(): jnp.dot(lax.all_gather(hidden, 'dp', axis=0, tiled=True), down_kept, pref...  21.2 us
    dot_general x1, matrix products, on_device(): up_part = jnp.dot(columns, up_kept, preferred_element_type=jnp.float32)  20.5 us
    all_gather x1, waiting for transfers between devices, on_device(): lax.all_gather(hidden, 'dp', axis=0, tiled=True)  17.7 us
  transfers between devices with their start and end apart: 4, of which 3 were waited for; matrix products, arithmetic and copies ran while one was open for 24% of the time, Pallas kernels for 0%

commit v1 on v0

--- a/solution.py
+++ b/solution.py
@@ -17,7 +17,10 @@
     values = tokens.astype(jnp.float32)
     scale = lax.rsqrt(jnp.mean(values * values, axis=1, keepdims=True) + 1e-05)
     normed = (values * scale * norm_gain).astype(jnp.bfloat16)
-    columns = lax.all_to_all(normed, "dp", split_axis=1, concat_axis=0, tiled=True)
+    columns = jnp.concatenate(
+        lax.all_to_all(jnp.stack(jnp.split(normed, lax.axis_size("dp"), axis=1)), "dp", 0, 0),
+        axis=0,
+    )
     widened = columns.astype(jnp.float32)
     input_norms = jnp.sqrt(jnp.sum(widened * widened, axis=0))
     gate_kept = keep_entries(gate_weight, gate_mask)

time: 452 us -> 440 us (0.973)
  local copies, waits for them, and re-layouts: 74.5 us -> 62.2 us
    unnamed x14 -> x9, local copies, waits for them, and re-layouts: 66.7 us -> 60.3 us
    all_to_all x1 -> x0, local copies, waits for them, and re-layouts: 6.33 us -> none  [on_device(): lax.all_to_all(normed, 'dp', split_axis=1, concat_axis=0, tiled=True)]
  transfers between devices with their start and end apart: 4 -> 4, of which waited for: 3 -> 3; matrix products, arithmetic and copies ran while one was open for 24% -> 25% of each run, Pallas kernels for 0% -> 0%
where the time goes in v1:
time: 440 us; the launch traced here: 438 us
  waiting for transfers between devices  208 us (47%)
  other arithmetic  73.5 us (17%)
  matrix products  64.7 us (15%)
  local copies, waits for them, and re-layouts  62.2 us (14%)
  between operations  13.8 us (3%)
  blocking collectives  10.6 us (2%)
  starting transfers between devices  5.01 us (1%)
    reduce_scatter x1, waiting for transfers between devices, on_device(): lax.psum_scatter(jnp.concatenate([gate_part, up_part], axis=1).astype(jnp...  117 us
    reduce_scatter x1, waiting for transfers between devices, on_device(): lax.psum_scatter(partial_out.astype(jnp.bfloat16), 'mp', scatter_dimensio...  73.5 us
    unnamed x9, local copies, waits for them, and re-layouts  60.3 us
    select_n x2, other arithmetic, keep_entries(): return jnp.where(kept_bits == 1, weight, jnp.zeros_like(weight))  43.4 us
    dot_general x1, matrix products, on_device(): gate_part = jnp.dot(columns, gate_kept, preferred_element_type=jnp.float32)  21.8 us
    dot_general x1, matrix products, on_device(): up_part = jnp.dot(columns, up_kept, preferred_element_type=jnp.float32)  21.7 us
    dot_general x1, matrix products, on_device(): jnp.dot(lax.all_gather(hidden, 'dp', axis=0, tiled=True), down_kept, pref...  21.2 us
    all_gather x1, waiting for transfers between devices, on_device(): lax.all_gather(hidden, 'dp', axis=0, tiled=True)  17.7 us
  transfers between devices with their start and end apart: 4, of which 3 were waited for; matrix products, arithmetic and copies ran while one was open for 25% of the time, Pallas kernels for 0%

profile of v1, /device:TPU:0, one launch (start us, length us, event | category | flops | bytes accessed | tf_op | source)
XLA Modules:
  0.0 438.3 jit_solution(2331683268427819935)
XLA Ops:
  7.2 3.1 fusion.9
  10.3 3.6 fusion.11
  13.9 0.5 slice_bitcast_fusion.3
  14.4 2.2 pad_maximum_fusion.1
  16.6 4.9 %all-to-all-start = ((bf16[4,256,2048]{2,1,0:T(8,128)(2,1)}), bf16[4,256,2048]{2,1,0:T(8,128)(2,1)}, u32[]{:S(2)}, u32[]{:S(2)}) async-start(bf16[4,256,2048]{2,1,0:T(8,128)(2,1)} %pad_maximum_fusion.1), calls=%async_computation | async-start | bytes 8388608 | tf_op jit(solution)/shard_map/all_to_all | solution.py:21
  21.5 0.0 reduce-scatter.3.cloned.1.call-start
  21.6 20.2 %copy.14 = bf16[2048,3584]{0,1:T(8,128)(2,1)} copy(bf16[2048,3584]{1,0:T(8,128)(2,1)} %param.10) | data formatting | bytes 29360128 | tf_op args[2]
  41.8 0.0 copy-start
  41.8 0.0 copy-start.1
  41.8 20.5 %copy.15 = bf16[2048,3584]{0,1:T(8,128)(2,1)} copy(bf16[2048,3584]{1,0:T(8,128)(2,1)} %param.12) | data formatting | bytes 29360128 | tf_op args[4]
  62.3 0.1 shift_right_arithmetic.63
  62.4 0.0 copy-done
  62.4 0.0 copy-done.1
  62.4 28.3 %fusion.6 = (bf16[2048,3584]{0,1:T(8,128)(2,1)}, bf16[2048,3584]{0,1:T(8,128)(2,1)}) fusion(bf16[2048,3584]{0,1:T(8,128)(2,1)} %copy.14, s32[3584]{0:T(1024)S(1)} %shift_right_arithmetic.63, s32[2048,112]{0,1:T(8,128)S(1)} %copy-done, bf16[2048,3584]{0,1:T(8,128)(2,1)} %copy.15, s32[2048,112]{0,1:T(8,128)S(1)} %copy-done.1), kind=kLoop, calls=%fused_computation.9 | loop fusion | flops 58720256 | bytes 60569600 | tf_op jit(solution)/shard_map/jit(_where)/select_n | solution.py:11
  90.8 0.0 all-to-all-done
  90.8 21.7 %convolution_convert_fusion = bf16[1024,3584]{1,0:T(8,128)(2,1)} fusion(bf16[1024,2048]{1,0:T(8,128)(2,1)} %bitcast.4, bf16[2048,3584]{0,1:T(8,128)(2,1)} %get-tuple-element.10), kind=kOutput, calls=%fused_computation.19 | convolution fusion | flops 15036055552 | bytes 26214400 | tf_op jit(solution)/shard_map/dot_general | solution.py:31
  112.5 21.8 %convolution_convert_fusion.1 = bf16[1024,3584]{1,0:T(8,128)(2,1)} fusion(bf16[1024,2048]{1,0:T(8,128)(2,1)} %bitcast.4, bf16[2048,3584]{0,1:T(8,128)(2,1)} %get-tuple-element.9), kind=kOutput, calls=%fused_computation.20 | convolution fusion | flops 15036055552 | bytes 26214400 | tf_op jit(solution)/shard_map/dot_general | solution.py:30
  134.3 12.6 %pad_maximum_fusion = bf16[1024,7168]{1,0:T(8,128)(2,1)} fusion(bf16[1024,3584]{1,0:T(8,128)(2,1)} %convolution_convert_fusion, bf16[1024,3584]{1,0:T(8,128)(2,1)} %convolution_convert_fusion.1), kind=kLoop, calls=%fused_computation.12 | loop fusion | flops 29360128 | bytes 29360128 | tf_op jit(solution)/shard_map/concatenate | solution.py:33
  146.9 0.0 reduce-scatter.3.cloned.1.call-update
  147.0 0.0 all-gather.2.cloned.1.call-start
  147.0 117.2 %reduce-scatter.3.cloned.1.call-done = bf16[256,7168]{1,0:T(8,128)(2,1)} async-done(((bf16[1024,7168]{1,0:T(8,128)(2,1)}), bf16[256,7168]{1,0:T(8,128)(2,1)}) %reduce-scatter.3.cloned.1.call-update) | async-done | bytes 3670032 | tf_op jit(solution)/shard_map/reduce_scatter | solution.py:32
  264.2 2.9 convert_element_type.25
  267.1 2.5 multiply_reduce_fusion.1
  269.6 0.0 all-gather.2.cloned.1.call-update
  269.7 0.0 copy-start.2
  269.7 0.0 reduce-scatter.5.cloned.1.call-start
  269.7 19.5 %copy.16 = bf16[3584,2048]{0,1:T(8,128)(2,1)} copy(bf16[3584,2048]{1,0:T(8,128)(2,1)} %param.14) | data formatting | bytes 29360128 | tf_op args[6]
  289.3 0.1 shift_right_arithmetic.72
  289.3 0.0 copy-done.2
  289.3 15.1 %fusion.8 = bf16[3584,2048]{0,1:T(8,128)(2,1)} fusion(bf16[3584,2048]{0,1:T(8,128)(2,1)} %copy.16, s32[2048]{0:T(1024)S(1)} %shift_right_arithmetic.72, s32[3584,64]{0,1:T(8,128)S(1)} %copy-done.2), kind=kLoop, calls=%fused_computation.11 | loop fusion | flops 29360128 | bytes 30285824 | tf_op jit(solution)/shard_map/jit(_where)/select_n | solution.py:11
  304.4 17.7 %all-gather.2.cloned.1.call-done = bf16[1024,3584]{1,0:T(8,128)(2,1)} async-done(((bf16[256,3584]{1,0:T(8,128)(2,1)}), bf16[1024,3584]{1,0:T(8,128)(2,1)}) %all-gather.2.cloned.1.call-update) | async-done | bytes 7340048 | tf_op jit(solution)/shard_map/all_gather | solution.py:43
  322.1 21.2 %convolution_convert_fusion.2 = bf16[1024,2048]{1,0:T(8,128)(2,1)} fusion(bf16[1024,3584]{1,0:T(8,128)(2,1)} %all-gather.2.cloned.1.call-done, bf16[3584,2048]{0,1:T(8,128)(2,1)} %fusion.8), kind=kOutput, calls=%fused_computation.22 | convolution fusion | flops 15034482688 | bytes 26214400 | tf_op jit(solution)/shard_map/dot_general | solution.py:42
  343.3 0.0 reduce-scatter.5.cloned.1.call-update
  343.4 3.1 multiply_reduce_fusion
  346.4 0.6 sqrt.6
  347.1 10.6 %psum.7 = f32[3584]{0:T(1024)S(1)} all-reduce(f32[3584]{0:T(1024)S(1)} %get-tuple-element.3), channel_id=1, replica_groups=mesh['dp'=4,'mp'=8] {'dp'}, use_global_device_ids=true, to_apply=%region_5.6 | all-reduce | flops 3584 | bytes 28672 | tf_op jit(solution)/shard_map/psum | solution.py:40
  357.7 0.6 sqrt.7
  358.3 73.5 %reduce-scatter.5.cloned.1.call-done = bf16[128,2048]{1,0:T(8,128)(2,1)} async-done(((bf16[1024,2048]{1,0:T(8,128)(2,1)}), bf16[128,2048]{1,0:T(8,128)(2,1)}) %reduce-scatter.5.cloned.1.call-update) | async-done | bytes 524304 | tf_op jit(solution)/shard_map/reduce_scatter | solution.py:47
  (3 shorter events, 0.0 us)
Async XLA Ops:
  16.6 74.1 %all-to-all-start = ((bf16[4,256,2048]{2,1,0:T(8,128)(2,1)}), bf16[4,256,2048]{2,1,0:T(8,128)(2,1)}, u32[]{:S(2)}, u32[]{:S(2)}) async-start(bf16[4,256,2048]{2,1,0:T(8,128)(2,1)} %pad_maximum_fusion.1), calls=%async_computation | async-start | bytes 8388608 | tf_op jit(solution)/shard_map/all_to_all | solution.py:21
  21.5 242.7 %reduce-scatter.3.cloned.1.call-start = ((), (), s32[]{:S(2)}) async-start(), calls=%async_computation.3 | async-start | bytes 18350080 | tf_op jit(solution)/shard_map/reduce_scatter | solution.py:32
  41.8 20.6 %copy-start = (s32[2048,112]{0,1:T(8,128)S(1)}, s32[2048,112]{0,1:T(8,128)}, u32[]{:S(2)}) copy-start(s32[2048,112]{0,1:T(8,128)} %param.11) | copy-start | bytes 2752516
  41.8 20.6 %copy-start.1 = (s32[2048,112]{0,1:T(8,128)S(1)}, s32[2048,112]{0,1:T(8,128)}, u32[]{:S(2)}) copy-start(s32[2048,112]{0,1:T(8,128)} %param.13) | copy-start | bytes 2752516
  147.0 175.2 %all-gather.2.cloned.1.call-start = ((), (), s32[]{:S(2)}) async-start(), calls=%async_computation.4 | async-start | bytes 9175040 | tf_op jit(solution)/shard_map/all_gather | solution.py:43
  269.7 19.7 %copy-start.2 = (s32[3584,64]{0,1:T(8,128)S(1)}, s32[3584,64]{0,1:T(8,128)}, u32[]{:S(2)}) copy-start(s32[3584,64]{0,1:T(8,128)} %param.15) | copy-start | bytes 2752516
  269.7 162.1 %reduce-scatter.5.cloned.1.call-start = ((), (), s32[]{:S(2)}) async-start(), calls=%async_computation.5 | async-start | bytes 4718592 | tf_op jit(solution)/shard_map/reduce_scatter | solution.py:47
Sparse Core Ops, SparseCore 0:
  147.1 117.0 reduce-scatter.2
  269.8 52.2 all-gather.1
  343.5 88.2 reduce-scatter.4
